TPU v7x, 32 devices: a whole 2x2x4 slice. The times are simulated.
32 devices in a mesh: shard: 4 (over z), replica: 8 (over y, x, core).
Axes of the slice: x: 2, y: 2, z: 4, core: 2. Of those that a mesh axis runs over, the one named last changes fastest.
Arguments:
- atom_feats: bfloat16 [2048, 9, 128], P(('shard', 'replica')), may hold values from -6 to 6
- cotangent: bfloat16 [2048, 9, 128], P(('shard', 'replica')), may hold values from -6 to 6
- frames: bfloat16 [9, 9, 8192], P(None, None, ('shard', 'replica')), may hold values from -2 to 2
- radial: bfloat16 [8192, 128], P(('shard', 'replica')), may hold values from 0.19921875 to 2
- edge_source: int32 [8192], P(('shard', 'replica')), may hold values from 0 to 63
- edge_target: int32 [8192], P(('shard', 'replica')), may hold values from 0 to 63
- edge_valid: int32 [8192], P(('shard', 'replica')), may hold values 0 or 1
- atom_types: int32 [2048], P(('shard', 'replica')), may hold values from 0 to 99
- dataset: int32 [32], P(('shard', 'replica')), may hold values from 0 to 4
- type_table: float32 [100, 128], replicated, may hold values from -6 to 6
- dataset_table: float32 [5, 128], replicated, may hold values from -6 to 6
- router_weight: float32 [128, 28], replicated, may hold values from -1.5 to 1.5
- experts: bfloat16 [28, 384, 384], P(None, 'shard'), may hold values from -3 to 3
Outputs:
- updated: bfloat16 [2048, 9, 128], P(('shard', 'replica'))
- feats_grad: float32 [2048, 9, 128], P(('shard', 'replica'))
- expert_grad: float32 [28, 384, 384], P(None, 'shard')
Inputs may be any that keep to these rules, and one draw needn't show every extreme that they name: `edge_source`: indices of atoms within the edge's own system. `edge_target`: indices of atoms within the edge's own system.
All inputs are finite; a program needn't handle non-finite values. No bound on the sum of `edge_valid` on one device may be relied on, other than what follows from the above.
Results may differ from a plain program's by a relative error of at most 0.011.
Values may be sent and summed in bfloat16 or wider, within the bound.
A program may use at most 64 MiB of HBM per device.

v0:
```python
import math
import jax
import jax.numpy as jnp
from jax import lax
from jax.sharding import PartitionSpec as P


def system_mix(type_rows, dataset_one, type_table, dataset_table, router_weight):
    table_size = type_table.shape[0]
    onehot = (type_rows[:, None] == jnp.arange(table_size, dtype=jnp.int32)[None, :]).astype(
        jnp.float32
    )
    counts = jnp.sum(onehot, axis=0)
    embed = jnp.dot(counts, type_table, precision=lax.Precision.HIGHEST) / type_rows.shape[0]
    pick = (
        dataset_one[:, None] == jnp.arange(dataset_table.shape[0], dtype=jnp.int32)[None, :]
    ).astype(jnp.float32)
    embed = embed + jnp.dot(pick, dataset_table, precision=lax.Precision.HIGHEST)[0]
    soft = jax.nn.softplus(jnp.dot(embed, router_weight, precision=lax.Precision.HIGHEST))
    return soft / jnp.sum(soft)


def edge_layer(feats32, merged32, frames, radial, source, target, valid):
    atom_count, components, channels = feats32.shape
    edge_count = source.shape[0]
    top_degree = math.isqrt(components) - 1
    feats = feats32.astype(jnp.bfloat16)
    merged = merged32.astype(jnp.bfloat16)
    gathered = jnp.take(feats, source, axis=0)
    rotated = jnp.einsum(
        "ije,ejc->eic", frames.astype(jnp.float32), gathered.astype(jnp.float32)
    ).astype(jnp.bfloat16)
    zero_rows = [degree * degree + degree for degree in range(top_degree + 1)]
    zero_band = jnp.concatenate(
        [rotated[:, row : row + 1, :] for row in zero_rows], axis=1
    ).reshape(edge_count, -1)
    mixed_band = jnp.dot(zero_band, merged, preferred_element_type=jnp.float32).reshape(
        edge_count, top_degree + 1, channels
    )
    columns = []
    for column in range(components):
        if column in zero_rows:
            columns.append(mixed_band[:, zero_rows.index(column), :])
        else:
            columns.append(rotated[:, column, :].astype(jnp.float32))
    combined = jnp.stack(columns, axis=1)
    message = (combined * radial.astype(jnp.float32)[:, None, :]).astype(jnp.bfloat16)
    unrotated = jnp.einsum(
        "jie,ejc->eic", frames.astype(jnp.float32), message.astype(jnp.float32)
    ).astype(jnp.bfloat16)
    incidence = (
        (target[None, :] == jnp.arange(atom_count, dtype=jnp.int32)[:, None]) & (valid[None, :] > 0)
    ).astype(jnp.bfloat16)
    summed = jnp.dot(
        incidence, unrotated.reshape(edge_count, -1), preferred_element_type=jnp.float32
    )
    return feats32 + summed.reshape(atom_count, components, channels) * (atom_count / edge_count)


def add_system(total, pair):
    mix_row, rows = pair
    term = lax.optimization_barrier((mix_row[:, None, None] * rows[None]).astype(jnp.bfloat16))
    return (total + term.astype(jnp.float32), None)


def shards(
    atom_feats,
    cotangent,
    frames,
    radial,
    edge_source,
    edge_target,
    edge_valid,
    atom_types,
    dataset,
    type_table,
    dataset_table,
    router_weight,
    experts,
):
    group = lax.axis_size("shard")
    row_block = experts.shape[1]
    row_total = row_block * group
    mixture = system_mix(atom_types, dataset, type_table, dataset_table, router_weight)
    group_mixtures = lax.all_gather(mixture[None, :], "shard", axis=0, tiled=True)
    row_shares = jnp.einsum(
        "sk,krc->src", group_mixtures, experts.astype(jnp.float32), precision=lax.Precision.HIGHEST
    ).astype(jnp.bfloat16)
    merged = lax.all_to_all(row_shares, "shard", split_axis=0, concat_axis=1, tiled=True).reshape(
        row_total, -1
    )
    merged32 = lax.optimization_barrier(merged).astype(jnp.float32)

    def local(feats32, weight32):
        return edge_layer(feats32, weight32, frames, radial, edge_source, edge_target, edge_valid)

    result, pullback = jax.vjp(local, atom_feats.astype(jnp.float32), merged32)
    feats_grad, weight_grad = pullback(cotangent.astype(jnp.float32))
    back_mixtures = lax.all_gather(mixture[None, :], "shard", axis=0, tiled=True)
    received = lax.all_to_all(
        weight_grad.reshape(group, row_block, -1).astype(jnp.bfloat16),
        "shard",
        split_axis=0,
        concat_axis=0,
        tiled=True,
    ).astype(jnp.float32)
    start = jnp.zeros(experts.shape, jnp.float32)
    shard_sum, unused = lax.scan(add_system, start, (back_mixtures, received))
    expert_grad = lax.psum(shard_sum, "replica")
    return (result.astype(jnp.bfloat16), feats_grad, expert_grad)


def solution(mesh):
    in_specs = (
        P(("shard", "replica"), None, None),
        P(("shard", "replica"), None, None),
        P(None, None, ("shard", "replica")),
        P(("shard", "replica"), None),
        P(("shard", "replica")),
        P(("shard", "replica")),
        P(("shard", "replica")),
        P(("shard", "replica")),
        P(("shard", "replica")),
        P(),
        P(),
        P(),
        P(None, "shard", None),
    )
    out_specs = (
        P(("shard", "replica"), None, None),
        P(("shard", "replica"), None, None),
        P(None, "shard", None),
    )
    return jax.shard_map(shards, mesh=mesh, in_specs=in_specs, out_specs=out_specs, check_vma=False)
```

profile of v0, /device:TPU:0, one launch (start us, length us, event | category | flops | bytes accessed | tf_op | source)
XLA Modules:
  0.0 189.4 jit_solution(16895955329291108513)
XLA Ops:
  8.0 0.7 convert_reduce_fusion
  8.8 1.2 dynamic-slice
  10.7 0.8 convolution_bitcast_fusion.1
  11.5 1.0 fusion.12
  12.5 1.5 fusion.55
  14.0 0.7 divide_dynamic-update-slice_fusion
  14.7 13.5 %all-reduce.11 = f32[112]{0:T(128)S(1)} all-reduce(f32[112]{0:T(128)S(1)} %divide_dynamic-update-slice_fusion), channel_id=2, replica_groups=mesh['shard'=4,'replica'=8] {'shard'}, use_global_device_ids=true, to_apply=%add.11 | all-reduce | flops 112 | bytes 896
  28.2 1.4 fusion.5
  29.6 0.7 copy.100
  30.4 3.5 %all-to-all-start = ((bf16[4,96,384]{2,1,0:T(8,128)(2,1)}), bf16[4,96,384]{2,1,0:T(8,128)(2,1)S(1)}, u32[]{:S(2)}, u32[]{:S(2)}) async-start(bf16[4,96,384]{2,1,0:T(8,128)(2,1)} %copy.100), calls=%async_computation | async-start | bytes 589824 | tf_op jit(solution)/shard_map/all_to_all | solution.py:89
  35.7 1.2 convolution_convert_fusion
  36.8 1.3 copy.109
  38.2 1.7 copy.110
  39.9 1.9 copy.97
  41.8 3.8 %gather_fusion = bf16[256,9,128]{2,0,1:T(8,128)(2,1)} fusion(bf16[64,9,128]{2,0,1:T(8,128)(2,1)S(1)} %copy-done.1, s32[1024]{0:T(1024)} %pad_clamp_fusion), kind=kCustom, calls=%fused_computation | custom fusion | bytes 1180672 | tf_op jit(solution)/shard_map/jvp(jit(_take))/gather | solution.py:29
  45.5 1.2 broadcast_select_fusion
  47.3 1.6 slice_convert_fusion
  48.9 1.2 pad_maximum_fusion
  50.0 1.8 copy.98
  51.8 2.6 %fusion.56 = (bf16[256,9,128]{2,1,0:T(8,128)(2,1)}, f32[256,9,128]{2,1,0:T(8,128)S(1)}) fusion(f32[256,128]{1,0:T(8,128)} %convert_element_type.132, bf16[256,9,128]{2,1,0:T(8,128)(2,1)} %copy.110, bf16[9,9,256]{1,0,2:T(8,128)(2,1)S(1)} %copy.97), kind=kOutput, calls=%fused_computation.91 | convolution fusion | flops 6488064 | bytes 2531840 | tf_op jit(solution)/shard_map/transpose(jvp(jie,ejc->eic))/dot_general | solution.py:48
  55.4 1.0 fusion.58
  56.4 5.0 %all-to-all-start.1 = ((bf16[4,96,384]{2,1,0:T(8,128)(2,1)}), bf16[4,96,384]{2,1,0:T(8,128)(2,1)}, u32[]{:S(2)}, u32[]{:S(2)}) async-start(bf16[4,96,384]{2,1,0:T(8,128)(2,1)} %bitcast.24), calls=%async_computation.1 | async-start | bytes 589824 | tf_op jit(solution)/shard_map/all_to_all | solution.py:100
  62.1 1.9 %copy.106 = bf16[9,9,256]{0,1,2:T(8,128)(2,1)S(1)} copy(bf16[9,9,256]{2,1,0:T(8,128)(2,1)} %param.17) | data formatting | bytes 82944 | tf_op args[2]
  64.0 4.0 %fusion.52 = (bf16[256,1,128]{2,1,0:T(2,128)(2,1)}, bf16[256,1,128]{2,1,0:T(2,128)(2,1)}, bf16[256,1,128]{2,1,0:T(2,128)(2,1)}, bf16[256,1,128]{2,1,0:T(2,128)(2...) fusion(bf16[256,9,128]{2,1,0:T(8,128)(2,1)} %get-tuple-element.74), kind=kLoop, calls=%fused_computation.87 | loop fusion | bytes 786432 | tf_op jit(solution)/shard_map/transpose(jvp())/unstack | solution.py:46
  68.1 0.9 copy.101
  69.0 1.8 convert_element_type.147
  70.8 25.5 %while.11 = (s32[]{:T(128)}, f32[28,96,384]{2,1,0:T(8,128)}, f32[4,28]{1,0:T(4,128)}, f32[4,96,384]{2,1,0:T(8,128)}, s32[]{:T(128)}, /*index=5*/s32[]{:T(128)}) while((s32[]{:T(128)}, f32[28,96,384]{2,1,0:T(8,128)}, f32[4,28]{1,0:T(4,128)}, f32[4,96,384]{2,1,0:T(8,128)}, s32[]{:T(128)}, /*index=5*/s32[]{:T(128)}) %tuple.48), condition=%wide.region_4.5_spmd.clone, body=%wide.region_3.4_spmd.clone.sunk | while | flops 5160963 | bytes 12829103 | solution.py:108
  71.4 0.9 dynamic-slice_bitcast_fusion.4
  72.9 2.7 %select_add_fusion.2 = f32[28,96,384]{2,1,0:T(8,128)} fusion(f32[28,96,384]{2,1,0:T(8,128)} %get-tuple-element.108, bf16[28,96,384]{2,1,0:T(8,128)(2,1)S(1)} %multiply_convert_fusion.4, pred[]{:T(512)S(6)} %compare.14), kind=kLoop, calls=%fused_computation.2.clone.1 | loop fusion | flops 3096576 | bytes 10321921 | tf_op jit(solution)/shard_map/while/body/eval_jaxpr/add | solution.py:63
  76.2 0.9 dynamic-slice_bitcast_fusion.4
  77.6 4.8 %select_add_fusion.2 = f32[28,96,384]{2,1,0:T(8,128)} fusion(f32[28,96,384]{2,1,0:T(8,128)} %get-tuple-element.108, bf16[28,96,384]{2,1,0:T(8,128)(2,1)S(1)} %multiply_convert_fusion.4, pred[]{:T(512)S(6)} %compare.14), kind=kLoop, calls=%fused_computation.2.clone.1 | loop fusion | flops 3096576 | bytes 10321921 | tf_op jit(solution)/shard_map/while/body/eval_jaxpr/add | solution.py:63
  83.1 0.9 dynamic-slice_bitcast_fusion.4
  84.5 4.8 %select_add_fusion.2 = f32[28,96,384]{2,1,0:T(8,128)} fusion(f32[28,96,384]{2,1,0:T(8,128)} %get-tuple-element.108, bf16[28,96,384]{2,1,0:T(8,128)(2,1)S(1)} %multiply_convert_fusion.4, pred[]{:T(512)S(6)} %compare.14), kind=kLoop, calls=%fused_computation.2.clone.1 | loop fusion | flops 3096576 | bytes 10321921 | tf_op jit(solution)/shard_map/while/body/eval_jaxpr/add | solution.py:63
  90.0 0.9 dynamic-slice_bitcast_fusion.4
  91.4 4.8 %select_add_fusion.2 = f32[28,96,384]{2,1,0:T(8,128)} fusion(f32[28,96,384]{2,1,0:T(8,128)} %get-tuple-element.108, bf16[28,96,384]{2,1,0:T(8,128)(2,1)S(1)} %multiply_convert_fusion.4, pred[]{:T(512)S(6)} %compare.14), kind=kLoop, calls=%fused_computation.2.clone.1 | loop fusion | flops 3096576 | bytes 10321921 | tf_op jit(solution)/shard_map/while/body/eval_jaxpr/add | solution.py:63
  96.3 1.4 fusion.57
  97.7 0.8 fusion.53
  98.4 7.0 %stack.2 = f32[256,9,128]{2,1,0:T(8,128)} concatenate(f32[256,1,128]{2,1,0:T(1,128)} %bitcast.98, f32[256,1,128]{2,1,0:T(1,128)} %get-tuple-element.62, f32[256,1,128]{2,1,0:T(1,128)} %bitcast.97, f32[256,1,128]{2,1,0:T(1,128)} %get-tuple-element.61, f32[256,1,128]{2,1,0:T(1,128)} %get-tuple-element.60, f32[256,1,128]{2,1,0:T(1,128)} %get-tuple-element.59, ...), dimensions={1} | concatenate | bytes 2359296 | tf_op jit(solution)/shard_map/jvp()/stack | solution.py:46
  105.4 3.0 %fusion.3 = bf16[256,9,128]{2,1,0:T(8,128)(2,1)} fusion(bf16[9,9,256]{0,1,2:T(8,128)(2,1)S(1)} %copy.106, f32[256,9,128]{2,1,0:T(8,128)} %stack.2, f32[256,128]{1,0:T(8,128)} %convert_element_type.132), kind=kOutput, calls=%fused_computation.16 | convolution fusion | flops 6193152 | bytes 1942016 | tf_op jit(solution)/shard_map/jvp(jie,ejc->eic)/dot_general | solution.py:48
  108.5 2.4 %copy.107 = bf16[256,9,128]{0,2,1:T(8,128)(2,1)} copy(bf16[256,9,128]{2,1,0:T(8,128)(2,1)} %fusion.3) | data formatting | bytes 1179648 | tf_op jit(solution)/shard_map/jvp()/convert_element_type | solution.py:50
  110.8 1.2 fusion.59
  112.5 0.8 copy.126
  113.3 3.9 %fusion.4 = bf16[256,9,128]{2,1,0:T(8,128)(2,1)S(1)} fusion(bf16[9,9,256]{0,1,2:T(8,128)(2,1)} %copy-done.2, bf16[256,1,128]{2,1,0:T(2,128)(2,1)} %copy.126, bf16[256,1,128]{2,1,0:T(2,128)(2,1)S(1)} %copy.125, bf16[256,1,128]{2,1,0:T(2,128)(2,1)S(1)} %copy.124, bf16[256,1,128]{2,1,0:T(2,128)(2,1)} %get-tuple-element.52, ...), kind=kOutput, calls=%fused_computation.17 | convolution fusion | flops 10911744 | bytes 1221120 | tf_op jit(solution)/shard_map/transpose(jvp(ije,ejc->eic))/dot_general | solution.py:30
  117.3 9.3 %scatter_fusion = bf16[64,9,128]{2,1,0:T(8,128)(2,1)S(1)} fusion(bf16[64,9,128]{2,1,0:T(8,128)(2,1)S(1)} %broadcast_in_dim.24, s32[256]{0:T(256)S(1)} %copy-done.8, bf16[256,9,128]{2,1,0:T(8,128)(2,1)S(1)} %fusion.4), kind=kCustom, calls=%fused_computation.1 | custom fusion | flops 294912 | bytes 1770496 | tf_op jit(solution)/shard_map/transpose(jvp(jit(_take)))/scatter-add | solution.py:29
  126.6 1.7 convert_add_fusion
  128.3 2.1 %fusion.9 = bf16[64,9,128]{2,0,1:T(8,128)(2,1)} fusion(bf16[256,9,128]{0,2,1:T(8,128)(2,1)} %copy.107, bf16[64,9,128]{2,0,1:T(8,128)(2,1)S(1)} %copy-done.1, s32[256]{0:T(256)S(1)} %copy-done.10, pred[256]{0:T(512)(128)(4,1)S(1)} %copy-done.12), kind=kOutput, calls=%fused_computation.23 | convolution fusion | flops 38076416 | bytes 886016 | tf_op jit(solution)/shard_map/jvp()/dot_general | solution.py:54
  130.4 47.8 %all-reduce.14.cloned.1.call-done = f32[28,96,384]{2,1,0:T(8,128)} async-done(((f32[28,96,384]{2,1,0:T(8,128)}), f32[28,96,384]{2,1,0:T(8,128)}) %all-reduce.14.cloned.1.call-update) | async-done | bytes 4128784 | tf_op jit(solution)/shard_map/psum | solution.py:109
  178.2 4.4 %copy.149 = f32[28,96,384]{2,1,0:T(8,128)} copy(f32[28,96,384]{2,1,0:T(8,128)} %all-reduce.14.cloned.1.call-done) | data formatting | bytes 8257536
  (66 shorter events, 9.0 us)
Async XLA Ops:
  7.2 21.1 %copy-start = (bf16[28,96,384]{2,1,0:T(8,128)(2,1)S(1)}, bf16[28,96,384]{2,1,0:T(8,128)(2,1)}, u32[]{:S(2)}) copy-start(bf16[28,96,384]{2,1,0:T(8,128)(2,1)} %param.27) | copy-start | bytes 6193156
  7.2 26.7 %copy-start.15 = (s32[256]{0:T(256)S(1)}, s32[256]{0:T(256)}, u32[]{:S(2)}) copy-start(s32[256]{0:T(256)} %param.19) | copy-start | bytes 3076
  7.2 27.1 %copy-start.17 = (s32[256]{0:T(256)S(1)}, s32[256]{0:T(256)}, u32[]{:S(2)}) copy-start(s32[256]{0:T(256)} %param.21) | copy-start | bytes 3076
  7.2 27.8 %copy-start.6 = (bf16[256,128]{1,0:T(8,128)(2,1)S(1)}, bf16[256,128]{1,0:T(8,128)(2,1)}, u32[]{:S(2)}) copy-start(bf16[256,128]{1,0:T(8,128)(2,1)} %param.18) | copy-start | bytes 196612
  7.2 28.4 %copy-start.9 = (s32[256]{0:T(256)S(1)}, s32[256]{0:T(256)}, u32[]{:S(2)}) copy-start(s32[256]{0:T(256)} %param.20) | copy-start | bytes 3076
  7.2 28.4 %copy-start.5 = (bf16[64,9,128]{2,0,1:T(8,128)(2,1)S(1)}, bf16[64,9,128]{2,0,1:T(8,128)(2,1)}, u32[]{:S(2)}) copy-start(bf16[64,9,128]{2,0,1:T(8,128)(2,1)} %param.16) | copy-start | bytes 442372
  28.2 6.2 %copy-start.13 = (f32[112]{0:T(128)}, f32[112]{0:T(128)S(1)}, u32[]{:S(2)}) copy-start(f32[112]{0:T(128)S(1)} %all-reduce.11) | copy-start | bytes 1348
  30.4 26.0 %all-to-all-start = ((bf16[4,96,384]{2,1,0:T(8,128)(2,1)}), bf16[4,96,384]{2,1,0:T(8,128)(2,1)S(1)}, u32[]{:S(2)}, u32[]{:S(2)}) async-start(bf16[4,96,384]{2,1,0:T(8,128)(2,1)} %copy.100), calls=%async_computation | async-start | bytes 589824 | tf_op jit(solution)/shard_map/all_to_all | solution.py:89
  34.3 1.3 copy-start.7
  34.4 1.3 copy-start.11
  36.8 4.9 %copy-start.1 = (bf16[64,9,128]{2,0,1:T(8,128)(2,1)S(1)}, bf16[64,9,128]{2,0,1:T(8,128)(2,1)}, u32[]{:S(2)}) copy-start(bf16[64,9,128]{2,0,1:T(8,128)(2,1)} %param.15) | copy-start | bytes 442372
  51.8 2.9 %copy-start.16 = (pred[3]{0:T(512)(128)(4,1)S(1)}, pred[3]{0:T(512)(128)(4,1)}, u32[]{:S(2)}) copy-start(pred[3]{0:T(512)(128)(4,1)} %constant.42.clone.1) | copy-start | bytes 13
  54.5 0.9 copy-start.3
  54.5 7.0 %copy-start.14 = (f32[112]{0:T(128)S(1)}, f32[112]{0:T(128)}, u32[]{:S(2)}) copy-start(f32[112]{0:T(128)} %copy-done.13) | copy-start | bytes 1348
  55.2 6.2 %copy-start.4 = (bf16[256,3,128]{0,2,1:T(8,128)(2,1)}, bf16[256,3,128]{0,2,1:T(8,128)(2,1)S(1)}, u32[]{:S(2)}) copy-start(bf16[256,3,128]{0,2,1:T(8,128)(2,1)S(1)} %copy.112) | copy-start | bytes 589828
  56.4 12.6 %all-to-all-start.1 = ((bf16[4,96,384]{2,1,0:T(8,128)(2,1)}), bf16[4,96,384]{2,1,0:T(8,128)(2,1)}, u32[]{:S(2)}, u32[]{:S(2)}) async-start(bf16[4,96,384]{2,1,0:T(8,128)(2,1)} %bitcast.24), calls=%async_computation.1 | async-start | bytes 589824 | tf_op jit(solution)/shard_map/all_to_all | solution.py:100
  61.4 116.7 %all-reduce.14.cloned.1.call-start = ((), (), s32[]{:S(2)}) async-start(), calls=%async_computation.2 | async-start | bytes 8257536 | tf_op jit(solution)/shard_map/psum | solution.py:109
  64.0 41.4 %copy-start.2 = (bf16[9,9,256]{0,1,2:T(8,128)(2,1)}, bf16[9,9,256]{0,1,2:T(8,128)(2,1)S(1)}, u32[]{:S(2)}) copy-start(bf16[9,9,256]{0,1,2:T(8,128)(2,1)S(1)} %copy.106) | copy-start | bytes 124420
  113.3 4.0 %copy-start.8 = (s32[256]{0:T(256)S(1)}, s32[256]{0:T(256)}, u32[]{:S(2)}) copy-start(s32[256]{0:T(256)} %copy-done.7) | copy-start | bytes 3076
  117.3 11.0 %copy-start.10 = (s32[256]{0:T(256)S(1)}, s32[256]{0:T(256)}, u32[]{:S(2)}) copy-start(s32[256]{0:T(256)} %param.20) | copy-start | bytes 3076
  117.3 11.0 %copy-start.12 = (pred[256]{0:T(512)(128)(4,1)S(1)}, pred[256]{0:T(512)(128)(4,1)}, u32[]{:S(2)}) copy-start(pred[256]{0:T(512)(128)(4,1)} %copy-done.11) | copy-start | bytes 772
Sparse Core Ops, SparseCore 0:
  96.4 81.6 all-reduce.13
where the time goes:
time: 191 us; the launch traced here: 189 us
  waiting for transfers between devices  47.8 us (25%)
  local copies, waits for them, and re-layouts  42.7 us (22%)
  other arithmetic  39.5 us (21%)
  matrix products  21.6 us (11%)
  between operations  15.8 us (8%)
  blocking collectives  13.5 us (7%)
  starting transfers between devices  8.5 us (4%)
    psum x1, waiting for transfers between devices, shards(): expert_grad = lax.psum(shard_sum, 'replica')  47.8 us
    add x4, other arithmetic, add_system(): return (total + term.astype(jnp.float32), None)  17.2 us
    unnamed x1, blocking collectives  13.5 us
    another operation x3, local copies, waits for them, and re-layouts, edge_layer(): combined = jnp.stack(columns, axis=1)  11.2 us
    unnamed x44, local copies, waits for them, and re-layouts  10.7 us
    scatter-add x1, other arithmetic, edge_layer(): gathered = jnp.take(feats, source, axis=0)  9.32 us
    mul x8, local copies, waits for them, and re-layouts, add_system(): mix_row[:, None, None] * rows[None]  6.35 us
    dot_general x2, matrix products, edge_layer(): jnp.einsum('jie,ejc->eic', frames.astype(jnp.float32), message.astype(jnp...  5.67 us
  transfers between devices with their start and end apart: 3, of which 1 were waited for; matrix products, arithmetic and copies ran while one was open for 34% of the time, Pallas kernels for 0%

commit v1 on v0

--- a/solution.py
+++ b/solution.py
@@ -106,7 +106,11 @@
     ).astype(jnp.float32)
     start = jnp.zeros(experts.shape, jnp.float32)
     shard_sum, unused = lax.scan(add_system, start, (back_mixtures, received))
-    expert_grad = lax.psum(shard_sum, "replica")
+    expert_grad = shard_sum
+    for hop in (1, 2, 4):
+        expert_grad = expert_grad + lax.ppermute(
+            expert_grad, "replica", [(dev, dev ^ hop) for dev in range(8)]
+        )
     return (result.astype(jnp.bfloat16), feats_grad, expert_grad)
 
 

time: 191 us -> 266 us (1.39)
  waiting for transfers between devices: 47.8 us -> 140 us
  local copies, waits for them, and re-layouts: 42.7 us -> 27.7 us
  between operations: 15.8 us -> 2.24 us
  other arithmetic: 39.5 us -> 50.1 us
  starting transfers between devices: 8.5 us -> 12.9 us
    ppermute x0 -> x3, waiting for transfers between devices: none -> 137 us  [shards(): lax.ppermute(expert_grad, 'replica', [(dev, dev ^ hop) for dev in range(8)])]
    psum x1 -> x0, waiting for transfers between devices: 47.8 us -> none  [shards(): expert_grad = lax.psum(shard_sum, 'replica')]
    add x0 -> x3, other arithmetic: none -> 11.1 us  [shards(): expert_grad + lax.ppermute(expert_grad, 'replica', [(dev, dev ^ hop) for...]
    mul x8, local copies, waits for them, and re-layouts: 6.35 us -> 0.07 us  [add_system(): mix_row[:, None, None] * rows[None]]
    unnamed x44 -> x41, local copies, waits for them, and re-layouts: 10.7 us -> 4.6 us
    all_to_all x1, waiting for transfers between devices: 0.01 us -> 3.14 us  [shards(): lax.all_to_all(row_shares, 'shard', split_axis=0, concat_axis=1, tiled=True)]
    ppermute x0 -> x3, starting transfers between devices: none -> 3.08 us  [shards(): lax.ppermute(expert_grad, 'replica', [(dev, dev ^ hop) for dev in range(8)])]
  transfers between devices with their start and end apart: 3 -> 5, of which waited for: 1 -> 4; matrix products, arithmetic and copies ran while one was open for 34% -> 17% of each run, Pallas kernels for 0% -> 0%
where the time goes in v1:
time: 266 us; the launch traced here: 265 us
  waiting for transfers between devices  140 us (53%)
  other arithmetic  50.1 us (19%)
  local copies, waits for them, and re-layouts  27.7 us (10%)
  matrix products  19.6 us (7%)
  starting transfers between devices  12.9 us (5%)
  blocking collectives  12.3 us (5%)
    ppermute x3, waiting for transfers between devices, shards(): lax.ppermute(expert_grad, 'replica', [(dev, dev ^ hop) for dev in range(8)])  137 us
    add x4, other arithmetic, add_system(): return (total + term.astype(jnp.float32), None)  17.2 us
    unnamed x1, blocking collectives  12.3 us
    another operation x3, local copies, waits for them, and re-layouts, edge_layer(): combined = jnp.stack(columns, axis=1)  11.1 us
    add x3, other arithmetic, shards(): expert_grad + lax.ppermute(expert_grad, 'replica', [(dev, dev ^ hop) for...  11.1 us
    scatter-add x1, other arithmetic, edge_layer(): gathered = jnp.take(feats, source, axis=0)  9.32 us
    all_to_all x1, starting transfers between devices, shards(): lax.all_to_all(weight_grad.reshape(group, row_block, -1).astype(jnp.bfloa...  6.35 us
    dot_general x2, matrix products, edge_layer(): jnp.einsum('jie,ejc->eic', frames.astype(jnp.float32), message.astype(jnp...  5.77 us
  transfers between devices with their start and end apart: 5, of which 4 were waited for; matrix products, arithmetic and copies ran while one was open for 17% of the time, Pallas kernels for 0%

profile of v1, /device:TPU:0, one launch (start us, length us, event | category | flops | bytes accessed | tf_op | source)
XLA Modules:
  0.0 264.7 jit_solution(13097486189877065902)
XLA Ops:
  0.7 0.9 compare_and_fusion
  2.2 0.7 broadcast_compare_fusion
  2.9 1.5 convert_element_type.132
  4.4 1.3 convolution_convert_fusion
  6.0 1.7 copy.110
  7.7 1.0 copy.97
  8.7 3.6 %gather_fusion = bf16[256,9,128]{2,0,1:T(8,128)(2,1)} fusion(bf16[64,9,128]{2,0,1:T(8,128)(2,1)S(1)} %copy-done.1, s32[1024]{0:T(1024)S(1)} %pad_clamp_fusion), kind=kCustom, calls=%fused_computation | custom fusion | bytes 1180672 | tf_op jit(solution)/shard_map/jvp(jit(_take))/gather | solution.py:29
  12.3 1.2 broadcast_select_fusion
  14.0 1.6 slice_convert_fusion
  15.6 1.2 pad_maximum_fusion
  16.8 1.1 copy.98
  17.9 2.7 %fusion.56 = (bf16[256,9,128]{2,1,0:T(8,128)(2,1)}, f32[256,9,128]{2,1,0:T(8,128)S(1)}) fusion(f32[256,128]{1,0:T(8,128)} %convert_element_type.132, bf16[256,9,128]{2,1,0:T(8,128)(2,1)} %copy.110, bf16[9,9,256]{1,0,2:T(8,128)(2,1)S(1)} %copy.97), kind=kOutput, calls=%fused_computation.91 | convolution fusion | flops 6488064 | bytes 2531840 | tf_op jit(solution)/shard_map/transpose(jvp(jie,ejc->eic))/dot_general | solution.py:48
  21.5 1.0 fusion.58
  22.5 6.3 %all-to-all-start.1 = ((bf16[4,96,384]{2,1,0:T(8,128)(2,1)}), bf16[4,96,384]{2,1,0:T(8,128)(2,1)S(1)}, u32[]{:S(2)}, u32[]{:S(2)}) async-start(bf16[4,96,384]{2,1,0:T(8,128)(2,1)} %bitcast.24), calls=%async_computation.1 | async-start | bytes 589824 | tf_op jit(solution)/shard_map/all_to_all | solution.py:100
  31.1 0.8 fusion.55
  31.9 0.7 divide_dynamic-update-slice_fusion
  32.7 12.3 %all-reduce.11 = f32[112]{0:T(128)S(1)} all-reduce(f32[112]{0:T(128)S(1)} %divide_dynamic-update-slice_fusion), channel_id=2, replica_groups=mesh['shard'=4,'replica'=8] {'shard'}, use_global_device_ids=true, to_apply=%add.11 | all-reduce | flops 112 | bytes 896
  45.1 19.3 %while.11 = (s32[]{:T(128)}, f32[28,96,384]{2,1,0:T(8,128)}, f32[4,28]{1,0:T(4,128)S(1)}, f32[4,96,384]{2,1,0:T(8,128)S(1)}, s32[]{:T(128)}, /*index=5*/s32[]{:T(128)}) while((s32[]{:T(128)}, f32[28,96,384]{2,1,0:T(8,128)}, f32[4,28]{1,0:T(4,128)S(1)}, f32[4,96,384]{2,1,0:T(8,128)S(1)}, s32[]{:T(128)}, /*index=5*/s32[]{:T(128)}) %tuple.48), condition=%wide.region_4.5_spmd.clone, body=%wide.region_3.4_spmd.clone.sunk | while | flops 5160963 | bytes 12829103 | solution.py:108
  45.7 2.7 %select_add_fusion.2 = f32[28,96,384]{2,1,0:T(8,128)} fusion(f32[28,96,384]{2,1,0:T(8,128)} %get-tuple-element.108, bf16[28,96,384]{2,1,0:T(8,128)(2,1)S(1)} %multiply_convert_fusion.4, pred[]{:T(512)S(6)} %compare.14), kind=kLoop, calls=%fused_computation.2.clone.1 | loop fusion | flops 3096576 | bytes 10321921 | tf_op jit(solution)/shard_map/while/body/eval_jaxpr/add | solution.py:63
  48.9 4.8 %select_add_fusion.2 = f32[28,96,384]{2,1,0:T(8,128)} fusion(f32[28,96,384]{2,1,0:T(8,128)} %get-tuple-element.108, bf16[28,96,384]{2,1,0:T(8,128)(2,1)S(1)} %multiply_convert_fusion.4, pred[]{:T(512)S(6)} %compare.14), kind=kLoop, calls=%fused_computation.2.clone.1 | loop fusion | flops 3096576 | bytes 10321921 | tf_op jit(solution)/shard_map/while/body/eval_jaxpr/add | solution.py:63
  54.2 4.8 %select_add_fusion.2 = f32[28,96,384]{2,1,0:T(8,128)} fusion(f32[28,96,384]{2,1,0:T(8,128)} %get-tuple-element.108, bf16[28,96,384]{2,1,0:T(8,128)(2,1)S(1)} %multiply_convert_fusion.4, pred[]{:T(512)S(6)} %compare.14), kind=kLoop, calls=%fused_computation.2.clone.1 | loop fusion | flops 3096576 | bytes 10321921 | tf_op jit(solution)/shard_map/while/body/eval_jaxpr/add | solution.py:63
  59.5 4.8 %select_add_fusion.2 = f32[28,96,384]{2,1,0:T(8,128)} fusion(f32[28,96,384]{2,1,0:T(8,128)} %get-tuple-element.108, bf16[28,96,384]{2,1,0:T(8,128)(2,1)S(1)} %multiply_convert_fusion.4, pred[]{:T(512)S(6)} %compare.14), kind=kLoop, calls=%fused_computation.2.clone.1 | loop fusion | flops 3096576 | bytes 10321921 | tf_op jit(solution)/shard_map/while/body/eval_jaxpr/add | solution.py:63
  64.4 7.3 %collective-permute-done = f32[28,96,384]{2,1,0:T(8,128)S(1)} collective-permute-done((f32[28,96,384]{2,1,0:T(8,128)}, f32[28,96,384]{2,1,0:T(8,128)S(1)}, u32[]{:S(2)}, u32[]{:S(2)}) %collective-permute-start) | collective-permute-done | bytes 4128800 | tf_op jit(solution)/shard_map/ppermute | solution.py:111
  71.7 2.7 %add.62 = f32[28,96,384]{2,1,0:T(8,128)S(1)} add(f32[28,96,384]{2,1,0:T(8,128)} %get-tuple-element.25, f32[28,96,384]{2,1,0:T(8,128)S(1)} %collective-permute-done) | non-fusion elementwise | flops 1032192 | bytes 12386304 | tf_op jit(solution)/shard_map/add | solution.py:111
  74.4 1.6 collective-permute-start.1
  76.0 89.7 %collective-permute-done.1 = f32[28,96,384]{2,1,0:T(8,128)S(1)} collective-permute-done((f32[28,96,384]{2,1,0:T(8,128)S(1)}, f32[28,96,384]{2,1,0:T(8,128)S(1)}, u32[]{:S(2)}, u32[]{:S(2)}) %collective-permute-start.1) | collective-permute-done | bytes 4128800 | tf_op jit(solution)/shard_map/ppermute | solution.py:111
  165.7 2.4 add.63
  168.1 1.5 collective-permute-start.2
  169.7 1.4 fusion.5
  171.1 0.7 copy.100
  171.9 3.5 %all-to-all-start = ((bf16[4,96,384]{2,1,0:T(8,128)(2,1)}), bf16[4,96,384]{2,1,0:T(8,128)(2,1)S(1)}, u32[]{:S(2)}, u32[]{:S(2)}) async-start(bf16[4,96,384]{2,1,0:T(8,128)(2,1)} %copy.100), calls=%async_computation | async-start | bytes 589824 | tf_op jit(solution)/shard_map/all_to_all | solution.py:89
  175.3 1.9 copy.106
  177.2 3.9 %fusion.52 = (bf16[256,1,128]{2,1,0:T(2,128)(2,1)}, bf16[256,1,128]{2,1,0:T(2,128)(2,1)}, bf16[256,1,128]{2,1,0:T(2,128)(2,1)}, bf16[256,1,128]{2,1,0:T(2,128)(2...) fusion(bf16[256,9,128]{2,1,0:T(8,128)(2,1)} %get-tuple-element.74), kind=kLoop, calls=%fused_computation.87 | loop fusion | bytes 786432 | tf_op jit(solution)/shard_map/transpose(jvp())/unstack | solution.py:46
  181.2 3.1 %all-to-all-done = bf16[4,96,384]{2,1,0:T(8,128)(2,1)S(1)} async-done(((bf16[4,96,384]{2,1,0:T(8,128)(2,1)}), bf16[4,96,384]{2,1,0:T(8,128)(2,1)S(1)}, u32[]{:S(2)}, u32[]{:S(2)}) %all-to-all-start) | async-done | bytes 294944 | tf_op jit(solution)/shard_map/all_to_all | solution.py:89
  184.3 0.9 copy.101
  185.2 1.4 fusion.57
  186.6 0.8 fusion.53
  187.4 6.9 %stack.2 = f32[256,9,128]{2,1,0:T(8,128)} concatenate(f32[256,1,128]{2,1,0:T(1,128)} %bitcast.98, f32[256,1,128]{2,1,0:T(1,128)} %get-tuple-element.62, f32[256,1,128]{2,1,0:T(1,128)} %bitcast.97, f32[256,1,128]{2,1,0:T(1,128)} %get-tuple-element.61, f32[256,1,128]{2,1,0:T(1,128)} %get-tuple-element.60, f32[256,1,128]{2,1,0:T(1,128)} %get-tuple-element.59, ...), dimensions={1} | concatenate | bytes 2359296 | tf_op jit(solution)/shard_map/jvp()/stack | solution.py:46
  194.3 3.1 %fusion.3 = bf16[256,9,128]{2,1,0:T(8,128)(2,1)} fusion(bf16[9,9,256]{0,1,2:T(8,128)(2,1)S(1)} %copy.106, f32[256,9,128]{2,1,0:T(8,128)} %stack.2, f32[256,128]{1,0:T(8,128)} %convert_element_type.132), kind=kOutput, calls=%fused_computation.16 | convolution fusion | flops 6193152 | bytes 1942016 | tf_op jit(solution)/shard_map/jvp(jie,ejc->eic)/dot_general | solution.py:48
  197.4 2.4 copy.107
  199.7 1.2 fusion.59
  201.4 0.8 copy.126
  202.2 3.9 %fusion.4 = bf16[256,9,128]{2,1,0:T(8,128)(2,1)S(1)} fusion(bf16[9,9,256]{0,1,2:T(8,128)(2,1)} %copy-done.2, bf16[256,1,128]{2,1,0:T(2,128)(2,1)} %copy.126, bf16[256,1,128]{2,1,0:T(2,128)(2,1)S(1)} %copy.125, bf16[256,1,128]{2,1,0:T(2,128)(2,1)S(1)} %copy.124, bf16[256,1,128]{2,1,0:T(2,128)(2,1)} %get-tuple-element.52, ...), kind=kOutput, calls=%fused_computation.17 | convolution fusion | flops 10911744 | bytes 1221120 | tf_op jit(solution)/shard_map/transpose(jvp(ije,ejc->eic))/dot_general | solution.py:30
  206.1 9.3 %scatter_fusion = bf16[64,9,128]{2,1,0:T(8,128)(2,1)S(1)} fusion(bf16[64,9,128]{2,1,0:T(8,128)(2,1)S(1)} %broadcast_in_dim.24, s32[256]{0:T(256)S(1)} %copy-done.9, bf16[256,9,128]{2,1,0:T(8,128)(2,1)S(1)} %fusion.4), kind=kCustom, calls=%fused_computation.1 | custom fusion | flops 294912 | bytes 1770496 | tf_op jit(solution)/shard_map/transpose(jvp(jit(_take)))/scatter-add | solution.py:29
  215.4 1.7 convert_add_fusion
  217.1 2.0 fusion.9
  219.2 39.6 %collective-permute-done.2 = f32[28,96,384]{2,1,0:T(8,128)} collective-permute-done((f32[28,96,384]{2,1,0:T(8,128)}, f32[28,96,384]{2,1,0:T(8,128)}, u32[]{:S(2)}, u32[]{:S(2)}) %collective-permute-start.2) | collective-permute-done | bytes 4128800 | tf_op jit(solution)/shard_map/ppermute | solution.py:111
  258.8 5.9 %add.64 = f32[28,96,384]{2,1,0:T(8,128)} add(f32[28,96,384]{2,1,0:T(8,128)} %add.63, f32[28,96,384]{2,1,0:T(8,128)} %collective-permute-done.2) | non-fusion elementwise | flops 1032192 | bytes 12386304 | tf_op jit(solution)/shard_map/add | solution.py:111
  (69 shorter events, 5.9 us)
Async XLA Ops:
  0.6 169.1 %copy-start = (bf16[28,96,384]{2,1,0:T(8,128)(2,1)S(1)}, bf16[28,96,384]{2,1,0:T(8,128)(2,1)}, u32[]{:S(2)}) copy-start(bf16[28,96,384]{2,1,0:T(8,128)(2,1)} %param.27) | copy-start | bytes 6193156
  0.6 7.0 %copy-start.5 = (bf16[9,9,256]{2,1,0:T(8,128)(2,1)S(1)}, bf16[9,9,256]{2,1,0:T(8,128)(2,1)}, u32[]{:S(2)}) copy-start(bf16[9,9,256]{2,1,0:T(8,128)(2,1)} %param.17) | copy-start | bytes 124420
  2.2 2.2 copy-start.8
  2.9 1.5 copy-start.12
  5.7 3.0 %copy-start.1 = (bf16[64,9,128]{2,0,1:T(8,128)(2,1)S(1)}, bf16[64,9,128]{2,0,1:T(8,128)(2,1)}, u32[]{:S(2)}) copy-start(bf16[64,9,128]{2,0,1:T(8,128)(2,1)} %param.15) | copy-start | bytes 442372
  17.9 3.5 %copy-start.3 = (bf16[256,3,128]{0,2,1:T(8,128)(2,1)}, bf16[256,3,128]{0,2,1:T(8,128)(2,1)S(1)}, u32[]{:S(2)}) copy-start(bf16[256,3,128]{0,2,1:T(8,128)(2,1)S(1)} %copy.98) | copy-start | bytes 589828
  17.9 3.0 %copy-start.14 = (pred[3]{0:T(512)(128)(4,1)S(1)}, pred[3]{0:T(512)(128)(4,1)}, u32[]{:S(2)}) copy-start(pred[3]{0:T(512)(128)(4,1)} %constant.42.clone.1) | copy-start | bytes 13
  20.6 8.8 %copy-start.15 = (s32[64]{0:T(128)S(1)}, s32[64]{0:T(128)}, u32[]{:S(2)}) copy-start(s32[64]{0:T(128)} %param.22) | copy-start | bytes 772
  20.6 8.9 %copy-start.16 = (u32[32]{0:T(128)S(1)}, u32[32]{0:T(128)}, u32[]{:S(2)}) copy-start(u32[32]{0:T(128)} %constant.68) | copy-start | bytes 388
  20.6 10.2 %copy-start.10 = (f32[5,128]{1,0:T(8,128)S(1)}, f32[5,128]{1,0:T(8,128)}, u32[]{:S(2)}) copy-start(f32[5,128]{1,0:T(8,128)} %param.25) | copy-start | bytes 7684
  20.6 10.3 %copy-start.6 = (f32[100,128]{1,0:T(8,128)S(1)}, f32[100,128]{1,0:T(8,128)}, u32[]{:S(2)}) copy-start(f32[100,128]{1,0:T(8,128)} %param.24) | copy-start | bytes 153604
  20.6 10.5 %copy-start.7 = (f32[128,28]{0,1:T(8,128)S(1)}, f32[128,28]{0,1:T(8,128)}, u32[]{:S(2)}) copy-start(f32[128,28]{0,1:T(8,128)} %param.26) | copy-start | bytes 43012
  21.4 23.7 %copy-start.4 = (bf16[256,3,128]{0,2,1:T(8,128)(2,1)}, bf16[256,3,128]{0,2,1:T(8,128)(2,1)S(1)}, u32[]{:S(2)}) copy-start(bf16[256,3,128]{0,2,1:T(8,128)(2,1)S(1)} %copy.112) | copy-start | bytes 589828
  22.5 22.6 %all-to-all-start.1 = ((bf16[4,96,384]{2,1,0:T(8,128)(2,1)}), bf16[4,96,384]{2,1,0:T(8,128)(2,1)S(1)}, u32[]{:S(2)}, u32[]{:S(2)}) async-start(bf16[4,96,384]{2,1,0:T(8,128)(2,1)} %bitcast.24), calls=%async_computation.1 | async-start | bytes 589824 | tf_op jit(solution)/shard_map/all_to_all | solution.py:100
  64.4 7.3 %collective-permute-start = (f32[28,96,384]{2,1,0:T(8,128)}, f32[28,96,384]{2,1,0:T(8,128)S(1)}, u32[]{:S(2)}, u32[]{:S(2)}) collective-permute-start(f32[28,96,384]{2,1,0:T(8,128)} %get-tuple-element.25), channel_id=1, source_target_pairs={{0,1},{1,0},{2,3},{3,2},{4,5},{5,4},{6,7},{7,6},{8,9},{9,8},{10,11... | collective-permute-start | bytes 12386312 | tf_op jit(solution)/shard_map/ppermute | solution.py:111
  74.4 91.3 %collective-permute-start.1 = (f32[28,96,384]{2,1,0:T(8,128)S(1)}, f32[28,96,384]{2,1,0:T(8,128)S(1)}, u32[]{:S(2)}, u32[]{:S(2)}) collective-permute-start(f32[28,96,384]{2,1,0:T(8,128)S(1)} %add.62), channel_id=1, source_target_pairs={{0,2},{1,3},{2,0},{3,1},{4,6},{5,7},{6,4},{7,5},{8,10},{9,11},{10,... | collective-permute-start | bytes 12386312 | tf_op jit(solution)/shard_map/ppermute | solution.py:111
  168.1 90.7 %collective-permute-start.2 = (f32[28,96,384]{2,1,0:T(8,128)}, f32[28,96,384]{2,1,0:T(8,128)}, u32[]{:S(2)}, u32[]{:S(2)}) collective-permute-start(f32[28,96,384]{2,1,0:T(8,128)} %add.63), channel_id=1, source_target_pairs={{0,4},{1,5},{2,6},{3,7},{4,0},{5,1},{6,2},{7,3},{8,12},{9,13},{10,... | collective-permute-start | bytes 12386312 | tf_op jit(solution)/shard_map/ppermute | solution.py:111
  171.9 12.4 %all-to-all-start = ((bf16[4,96,384]{2,1,0:T(8,128)(2,1)}), bf16[4,96,384]{2,1,0:T(8,128)(2,1)S(1)}, u32[]{:S(2)}, u32[]{:S(2)}) async-start(bf16[4,96,384]{2,1,0:T(8,128)(2,1)} %copy.100), calls=%async_computation | async-start | bytes 589824 | tf_op jit(solution)/shard_map/all_to_all | solution.py:89
  177.2 17.1 %copy-start.2 = (bf16[9,9,256]{0,1,2:T(8,128)(2,1)}, bf16[9,9,256]{0,1,2:T(8,128)(2,1)S(1)}, u32[]{:S(2)}) copy-start(bf16[9,9,256]{0,1,2:T(8,128)(2,1)S(1)} %copy.106) | copy-start | bytes 124420
  202.2 3.9 %copy-start.9 = (s32[256]{0:T(256)S(1)}, s32[256]{0:T(256)}, u32[]{:S(2)}) copy-start(s32[256]{0:T(256)} %copy-done.8) | copy-start | bytes 3076
  206.1 11.0 %copy-start.11 = (s32[256]{0:T(256)S(1)}, s32[256]{0:T(256)}, u32[]{:S(2)}) copy-start(s32[256]{0:T(256)} %param.20) | copy-start | bytes 3076
  206.1 11.0 %copy-start.13 = (pred[256]{0:T(512)(128)(4,1)S(1)}, pred[256]{0:T(512)(128)(4,1)}, u32[]{:S(2)}) copy-start(pred[256]{0:T(512)(128)(4,1)} %copy-done.12) | copy-start | bytes 772
